TPU v7x, 32 devices: a whole 2x2x4 slice. The times are simulated.
32 devices in a mesh: fsdp: 16 (over z, y, x), model: 2 (over core).
Axes of the slice: x: 2, y: 2, z: 4, core: 2. Of those that a mesh axis runs over, the one named last changes fastest.
Arguments:
- train_query: float32 [2560, 4096], P('fsdp', 'model'), may hold values from -0.15625 to 0.15625
- drift_query: float32 [2560, 4096], P('fsdp', 'model'), may hold values from -6 to 6
- spread_query: float32 [2560, 4096], P('fsdp', 'model'), may hold values from 0.1 to 10
- train_key: float32 [2560, 1024], P('fsdp', 'model'), may hold values from -0.15625 to 0.15625
- drift_key: float32 [2560, 1024], P('fsdp', 'model'), may hold values from -6 to 6
- spread_key: float32 [2560, 1024], P('fsdp', 'model'), may hold values from 0.1 to 10
- train_value: float32 [2560, 1024], P('fsdp', 'model'), may hold values from -0.15625 to 0.15625
- drift_value: float32 [2560, 1024], P('fsdp', 'model'), may hold values from -6 to 6
- spread_value: float32 [2560, 1024], P('fsdp', 'model'), may hold values from 0.1 to 10
- norm_train: float32 [2560], P(('fsdp', 'model')), may hold values from 0.25 to 1.75
- norm_step: float32 [2560], P(('fsdp', 'model')), may hold values from -0.3 to 0.3
Outputs:
- serve_query: bfloat16 [2560, 4096], P(None, 'model')
- serve_key: bfloat16 [2560, 1024], P(None, 'model')
- serve_value: bfloat16 [2560, 1024], P(None, 'model')
- factor_query: float32 [4096], P('model')
- factor_key: float32 [1024], P('model')
- factor_value: float32 [1024], P('model')
- serve_norm: bfloat16 [2560], replicated
- fresh_query: float32 [2560, 4096], P('fsdp', 'model')
- fresh_key: float32 [2560, 1024], P('fsdp', 'model')
- fresh_value: float32 [2560, 1024], P('fsdp', 'model')
All inputs are finite; a program needn't handle non-finite values. Where the computation divides by a largest or mean magnitude, that divisor is 1e-20 or more.
Results may differ from a plain program's by a relative error of at most 0.001.
Values may be sent and summed in bfloat16 or wider, within the bound.
A program may use at most 64 MiB of HBM per device.

v0:
```python
import jax
import jax.numpy as jnp
from jax import lax
from jax.sharding import PartitionSpec as P

learn_rate = 0.02
decay_rate = 0.05
tiny_value = 1e-08


def per_device(
    train_query,
    drift_query,
    spread_query,
    train_key,
    drift_key,
    spread_key,
    train_value,
    drift_value,
    spread_value,
    norm_train,
    norm_step,
):
    fresh_query = train_query - learn_rate * (
        drift_query / (jnp.sqrt(spread_query) + tiny_value) + decay_rate * train_query
    )
    fresh_key = train_key - learn_rate * (
        drift_key / (jnp.sqrt(spread_key) + tiny_value) + decay_rate * train_key
    )
    fresh_value = train_value - learn_rate * (
        drift_value / (jnp.sqrt(spread_value) + tiny_value) + decay_rate * train_value
    )
    factor_query, factor_key, factor_value = lax.pmax(
        (
            jnp.max(jnp.abs(fresh_query), axis=0),
            jnp.max(jnp.abs(fresh_key), axis=0),
            jnp.max(jnp.abs(fresh_value), axis=0),
        ),
        "fsdp",
    )
    narrow_query, narrow_key, narrow_value = (
        (fresh_query / factor_query).astype(jnp.bfloat16),
        (fresh_key / factor_key).astype(jnp.bfloat16),
        (fresh_value / factor_value).astype(jnp.bfloat16),
    )
    serve_query, serve_key, serve_value = (
        lax.all_gather(narrow_query, "fsdp", axis=0, tiled=True),
        lax.all_gather(narrow_key, "fsdp", axis=0, tiled=True),
        lax.all_gather(narrow_value, "fsdp", axis=0, tiled=True),
    )
    serve_norm = lax.all_gather(
        (norm_train + norm_step).astype(jnp.bfloat16), ("fsdp", "model"), axis=0, tiled=True
    )
    return (
        serve_query,
        serve_key,
        serve_value,
        factor_query,
        factor_key,
        factor_value,
        serve_norm,
        fresh_query,
        fresh_key,
        fresh_value,
    )


def solution(mesh):
    in_specs = (
        P("fsdp", "model"),
        P("fsdp", "model"),
        P("fsdp", "model"),
        P("fsdp", "model"),
        P("fsdp", "model"),
        P("fsdp", "model"),
        P("fsdp", "model"),
        P("fsdp", "model"),
        P("fsdp", "model"),
        P(("fsdp", "model")),
        P(("fsdp", "model")),
    )
    out_specs = (
        P(None, "model"),
        P(None, "model"),
        P(None, "model"),
        P("model"),
        P("model"),
        P("model"),
        P(),
        P("fsdp", "model"),
        P("fsdp", "model"),
        P("fsdp", "model"),
    )
    return jax.shard_map(
        per_device, mesh=mesh, in_specs=in_specs, out_specs=out_specs, check_vma=False
    )
```

profile of v0, /device:TPU:0, one launch (start us, length us, event | category | flops | bytes accessed | tf_op | source)
XLA Modules:
  0.0 370.3 jit_solution(16772706034378925687)
XLA Ops:
  7.2 0.0 copy-start.5
  7.2 0.0 copy-start.6
  7.2 0.0 copy-start.7
  7.2 0.0 copy-start.8
  7.2 0.0 all-gather.6.cloned.1.call-start
  7.3 0.0 copy-start.9
  7.3 2.9 abs_reduce_fusion
  10.2 0.0 copy-start
  10.2 0.3 abs_reduce_fusion.1
  10.6 0.0 copy-start.3
  10.6 0.0 copy-start.4
  10.6 78.6 %all-reduce.1 = (f32[2048]{0:T(1024)S(1)}, f32[512]{0:T(512)S(1)}, f32[512]{0:T(512)S(1)}) all-reduce(f32[2048]{0:T(1024)S(1)} %get-tuple-element.17, f32[512]{0:T(512)S(1)} %get-tuple-element.19, f32[512]{0:T(512)S(1)} %get-tuple-element.13), channel_id=1, replica_groups=mesh['fsdp'=16,'model'=2] {'fsdp'}, use_global_device_ids=true, to_apply=%region_1.0 | all-reduce | flops 3072 | bytes 24576 | tf_op jit(solution)/shard_map/pmax | solution.py:33
  89.2 0.7 divide_convert_fusion.2
  89.9 0.0 all-gather.6.cloned.1.call-update
  89.9 0.0 all-gather.8.cloned.1.call-start
  90.0 0.7 divide_convert_fusion.1
  90.7 0.0 all-gather.8.cloned.1.call-update
  90.7 0.0 all-gather.4.cloned.1.call-start
  90.7 0.0 copy-start.14
  90.8 0.0 copy-start.15
  90.8 1.0 divide_convert_fusion
  91.7 0.0 copy-done.11
  91.7 0.0 all-gather.4.cloned.1.call-update
  91.8 0.2 dynamic-update-slice
  92.1 37.3 %all-reduce = bf16[2560]{0:T(1024)(128)(2,1)} all-reduce(bf16[2560]{0:T(1024)(128)(2,1)S(1)} %dynamic-update-slice), channel_id=1, replica_groups=mesh['fsdp'=16,'model'=2] {'fsdp','model'}, use_global_device_ids=true, to_apply=%add | all-reduce | flops 2560 | bytes 10240
  129.3 20.8 %all-gather.6.cloned.1.call-done = bf16[2560,512]{1,0:T(8,128)(2,1)} async-done(((bf16[160,512]{1,0:T(8,128)(2,1)}), bf16[2560,512]{1,0:T(8,128)(2,1)}) %all-gather.6.cloned.1.call-update) | async-done | bytes 2621456 | tf_op jit(solution)/shard_map/all_gather | solution.py:48
  150.1 65.8 %all-gather.8.cloned.1.call-done = bf16[2560,512]{1,0:T(8,128)(2,1)} async-done(((bf16[160,512]{1,0:T(8,128)(2,1)}), bf16[2560,512]{1,0:T(8,128)(2,1)}) %all-gather.8.cloned.1.call-update) | async-done | bytes 2621456 | tf_op jit(solution)/shard_map/all_gather | solution.py:49
  215.9 133.3 %all-gather.4.cloned.1.call-done = bf16[2560,2048]{1,0:T(8,128)(2,1)} async-done(((bf16[160,2048]{1,0:T(8,128)(2,1)}), bf16[2560,2048]{1,0:T(8,128)(2,1)}) %all-gather.4.cloned.1.call-update) | async-done | bytes 10485776 | tf_op jit(solution)/shard_map/all_gather | solution.py:47
  349.1 10.4 %copy.25 = bf16[2560,2048]{1,0:T(8,128)(2,1)} copy(bf16[2560,2048]{1,0:T(8,128)(2,1)} %all-gather.4.cloned.1.call-done) | data formatting | bytes 20971520
  359.6 1.5 copy.26
  361.1 1.2 copy-done.2
  362.3 1.5 copy.27
  (22 shorter events, 0.0 us)
Async XLA Ops:
  7.2 3.0 copy-start.5
  7.2 3.0 copy-start.6
  7.2 3.0 copy-start.7
  7.2 3.0 copy-start.8
  7.2 142.9 %all-gather.6.cloned.1.call-start = ((), (), s32[]{:S(2)}) async-start(), calls=%async_computation.1 | async-start | bytes 2785280 | tf_op jit(solution)/shard_map/all_gather | solution.py:48
  7.3 2.9 copy-start.9
  7.3 2.9 copy-start.10
  10.2 80.5 %copy-start = (f32[160,2048]{1,0:T(8,128)}, f32[160,2048]{1,0:T(8,128)S(1)}, u32[]{:S(2)}) copy-start(f32[160,2048]{1,0:T(8,128)S(1)} %get-tuple-element.38) | copy-start | bytes 3932164
  10.6 81.2 %copy-start.3 = (f32[160,512]{1,0:T(8,128)}, f32[160,512]{1,0:T(8,128)S(1)}, u32[]{:S(2)}) copy-start(f32[160,512]{1,0:T(8,128)S(1)} %get-tuple-element.40) | copy-start | bytes 983044
  10.6 81.1 %copy-start.4 = (f32[160,512]{1,0:T(8,128)}, f32[160,512]{1,0:T(8,128)S(1)}, u32[]{:S(2)}) copy-start(f32[160,512]{1,0:T(8,128)S(1)} %get-tuple-element.39) | copy-start | bytes 983044
  89.2 2.5 copy-start.11
  89.2 2.5 copy-start.12
  89.2 2.5 copy-start.13
  89.9 126.0 %all-gather.8.cloned.1.call-start = ((), (), s32[]{:S(2)}) async-start(), calls=%async_computation.2 | async-start | bytes 2785280 | tf_op jit(solution)/shard_map/all_gather | solution.py:49
  90.7 258.5 %all-gather.4.cloned.1.call-start = ((), (), s32[]{:S(2)}) async-start(), calls=%async_computation | async-start | bytes 11141120 | tf_op jit(solution)/shard_map/all_gather | solution.py:47
  90.7 1.0 copy-start.14
  90.8 1.0 copy-start.15
  349.1 10.4 %copy-start.1 = (bf16[2560,512]{1,0:T(8,128)(2,1)S(1)}, bf16[2560,512]{1,0:T(8,128)(2,1)}, u32[]{:S(2)}) copy-start(bf16[2560,512]{1,0:T(8,128)(2,1)} %all-gather.6.cloned.1.call-done) | copy-start | bytes 7864324
  359.6 2.7 copy-start.2
Sparse Core Ops, SparseCore 0:
  90.0 60.0 all-gather.5
  153.4 62.4 all-gather.7
  219.1 129.9 all-gather.3
where the time goes:
time: 371 us; the launch traced here: 370 us
  waiting for transfers between devices  220 us (59%)
  blocking collectives  116 us (31%)
  local copies, waits for them, and re-layouts  14.9 us (4%)
  between operations  14 us (4%)
  other arithmetic  5.56 us (1%)
    all_gather x1, waiting for transfers between devices, per_device(): lax.all_gather(narrow_query, 'fsdp', axis=0, tiled=True)  133 us
    pmax x1, blocking collectives, per_device(): lax.pmax((jnp.max(jnp.abs(fresh_query), axis=0), jnp.max(jnp.abs(fresh_ke...  78.6 us
    all_gather x1, waiting for transfers between devices, per_device(): lax.all_gather(narrow_value, 'fsdp', axis=0, tiled=True)  65.8 us
    unnamed x1, blocking collectives  37.3 us
    all_gather x1, waiting for transfers between devices, per_device(): lax.all_gather(narrow_key, 'fsdp', axis=0, tiled=True)  20.8 us
    unnamed x37, local copies, waits for them, and re-layouts  14.9 us
  transfers between devices with their start and end apart: 3, of which 3 were waited for; matrix products, arithmetic and copies ran while one was open for 1% of the time, Pallas kernels for 0%

commit v1 on v0

--- a/solution.py
+++ b/solution.py
@@ -1,11 +1,342 @@
+import functools
+
 import jax
 import jax.numpy as jnp
 from jax import lax
+from jax.experimental import pallas as pl
+from jax.experimental.pallas import tpu as pltpu
 from jax.sharding import PartitionSpec as P
 
 learn_rate = 0.02
 decay_rate = 0.05
 tiny_value = 1e-08
+MESH = pl.DeviceIdType.MESH
+ROWS = 16
+LANES = 128
+
+AZ, BZ, AX, AXF, AY, AYF, BX, BXF, BY, BYF, COUNT = 0, 4, 20, 24, 28, 32, 36, 37, 38, 39, 40
+
+
+def stepped(train, drift, spread):
+    return train - learn_rate * (drift / (jnp.sqrt(spread) + tiny_value) + decay_rate * train)
+
+
+def gather_kernel(
+    part_a, fresh_q, fresh_k, fresh_v, norm_row, held, factor, norms,
+    mx, mx_send, mx_recv, nm_send, nm_recv, send, recv,
+):
+    f = lax.axis_index("fsdp")
+    m = lax.axis_index("model")
+    z = f // 4
+    r = f % 4
+    y = r // 2
+    x = r % 2
+    rx, ry, rd = y * 2 + (1 - x), (1 - y) * 2 + x, (1 - y) * 2 + (1 - x)
+    rows = fresh_q.shape[0]
+    widths = (fresh_q.shape[1], fresh_k.shape[1], fresh_v.shape[1])
+    starts = (0, widths[0], widths[0] + widths[1])
+    fresh = (fresh_q, fresh_k, fresh_v)
+    half_a = part_a // 2
+    half_b = (rows - part_a) // 2
+
+    def device(zz, rr):
+        return {"fsdp": zz * 4 + rr, "model": m}
+
+    plane = [device(z, rx), device(z, ry), device(z, rd)]
+    line = [device((z + k) % 4, r) for k in range(1, 4)]
+    partner = {"fsdp": f, "model": 1 - m}
+
+    barrier = pltpu.get_barrier_semaphore()
+    for peer in plane + line + [partner]:
+        pl.semaphore_signal(barrier, inc=1, device_id=peer, device_id_type=MESH)
+
+    for ref, start, width in zip(fresh, starts, widths):
+        step = min(512, width)
+        for c in range(0, width, step):
+            def body(i, acc, ref=ref, c=c, step=step):
+                return jnp.maximum(acc, jnp.abs(ref[pl.ds(i * 8, 8), c : c + step]))
+            acc = lax.fori_loop(0, rows // 8, body, jnp.zeros((8, step), jnp.float32), unroll=4)
+            mx[0, :, start + c : start + c + step] = jnp.max(acc, axis=0, keepdims=True)
+    norms[m, f] = norm_row[...]
+
+    pl.semaphore_wait(barrier, 7)
+
+    def remote(src, dst, s, d, peer):
+        return pltpu.make_async_remote_copy(
+            src_ref=src, dst_ref=dst, send_sem=s, recv_sem=d, device_id=peer, device_id_type=MESH
+        )
+
+    small = []
+    for k, peer in enumerate(plane):
+        copy = remote(mx.at[0], mx.at[1 + k], mx_send.at[k], mx_recv.at[k], peer)
+        copy.start()
+        small.append(copy)
+    tags = []
+    for k, peer in enumerate(plane):
+        copy = remote(norms.at[m, f], norms.at[m, f], nm_send.at[k], nm_recv.at[k], peer)
+        copy.start()
+        tags.append(copy)
+    for copy in small:
+        copy.wait_recv()
+    mx[4] = jnp.maximum(jnp.maximum(mx[0], mx[1]), jnp.maximum(mx[2], mx[3]))
+    for k, peer in enumerate(line):
+        copy = remote(mx.at[4], mx.at[5 + k], mx_send.at[3 + k], mx_recv.at[3 + k], peer)
+        copy.start()
+        small.append(copy)
+    for k, rr in enumerate((rx, ry, rd)):
+        mine = norms.at[m, z * 4 + rr]
+        remote(mine, mine, nm_send.at[k], nm_recv.at[k], plane[k]).wait_recv()
+    group = norms.at[m, pl.ds(z * 4, 4)]
+    for k, peer in enumerate(line):
+        copy = remote(group, group, nm_send.at[3 + k], nm_recv.at[3 + k], peer)
+        copy.start()
+        tags.append(copy)
+    for copy in small[3:]:
+        copy.wait_recv()
+    factor[...] = jnp.maximum(jnp.maximum(mx[4], mx[5]), jnp.maximum(mx[6], mx[7]))
+
+    def narrow(first, last):
+        def body(i, carry):
+            at = pl.ds(pl.multiple_of(first + i * ROWS, ROWS), ROWS)
+            for ref, start, width in zip(fresh, starts, widths):
+                step = min(512, width)
+                for c in range(0, width, step):
+                    scale = factor[:, start + c : start + c + step]
+                    held[f, at, start + c : start + c + step] = (
+                        ref[at, c : c + step] / scale
+                    ).astype(jnp.bfloat16)
+            return carry
+        lax.fori_loop(0, (last - first) // ROWS, body, 0)
+
+    done = []
+
+    def piece(zz, rr, first, last):
+        return held.at[zz * 4 + rr, pl.ds(first, last - first)]
+
+    def copy_of(zz, rr, first, last, s, d, peer):
+        block = piece(zz, rr, first, last)
+        return remote(block, block, send.at[s], recv.at[d], peer)
+
+    def go(make):
+        make().start()
+        done.append(make)
+
+    def got(zz, rr, first, last, d):
+        copy_of(zz, rr, first, last, d, d, plane[0]).wait_recv()
+
+    hi = z // 2
+    z_end, z_mid, z_mid2, z_end2 = 3 * hi, 1 + hi, 2 - hi, 3 - 3 * hi
+    is_end = z == z_end
+    is_mid = z == z_mid
+    near = z_end + z_mid - z
+    plane_of = (r, rx, ry, rd)
+
+    def az(zz, to, outward):
+        go(lambda: copy_of(zz, r, 0, part_a, AZ + zz + (COUNT if outward else 0), AZ + zz, device(to, r)))
+
+    def bz(zz, j, to, outward):
+        def make():
+            at = BZ + zz * 4 + j
+            back = at + (COUNT if outward else 0)
+            return copy_of(zz, plane_of[j], part_a, rows, back, at, device(to, r))
+        go(make)
+
+    def got_az(zz):
+        got(zz, r, 0, part_a, AZ + zz)
+
+    def got_bz(zz, j):
+        got(zz, plane_of[j], part_a, rows, BZ + zz * 4 + j)
+
+    def a_own(zz):
+        go(lambda: copy_of(zz, r, 0, part_a, AX + zz, AX + zz, plane[0]))
+        go(lambda: copy_of(zz, r, 0, part_a, AY + zz, AY + zz, plane[1]))
+
+    def a_forward(zz):
+        got(zz, rx, 0, part_a, AX + zz)
+        go(lambda: copy_of(zz, rx, half_a, part_a, AYF + zz, AYF + zz, plane[1]))
+        got(zz, ry, 0, part_a, AY + zz)
+        go(lambda: copy_of(zz, ry, 0, half_a, AXF + zz, AXF + zz, plane[0]))
+
+    narrow(part_a, rows)
+    go(lambda: copy_of(z, r, part_a, rows, BX, BX, plane[0]))
+    go(lambda: copy_of(z, r, part_a, rows, BY, BY, plane[1]))
+    narrow(0, part_a)
+
+    tail = []
+
+    def branch(pred):
+        def wrap(body):
+            @pl.when(pred)
+            def _():
+                kept = list(done)
+                done.clear()
+                body()
+                tail.append((pred, list(done)))
+                done.clear()
+                done.extend(kept)
+        return wrap
+
+    @branch(is_end)
+    def _():
+        az(z_end, z_mid, False)
+
+    @branch(is_mid)
+    def _():
+        az(z_mid, z_mid2, False)
+        az(z_mid, z_end, True)
+
+    a_own(z)
+    got(z, rx, part_a, rows, BX)
+    go(lambda: copy_of(z, rx, part_a + half_b, rows, BYF, BYF, plane[1]))
+    got(z, ry, part_a, rows, BY)
+    go(lambda: copy_of(z, ry, part_a, part_a + half_b, BXF, BXF, plane[0]))
+
+    @branch(is_end)
+    def _():
+        for j in (0, 1):
+            bz(z_end, j, z_mid, False)
+        got_az(z_mid)
+
+    @branch(is_mid)
+    def _():
+        for j in (0, 1):
+            bz(z_mid, j, z_mid2, False)
+            bz(z_mid, j, z_end, True)
+        got_az(z_end)
+        az(z_end, z_mid2, False)
+        got_az(z_mid2)
+        az(z_mid2, z_end, True)
+
+    a_own(near)
+    got(z, rd, part_a, part_a + half_b, BXF)
+    got(z, rd, part_a + half_b, rows, BYF)
+
+    @branch(is_end)
+    def _():
+        for j in (2, 3):
+            bz(z_end, j, z_mid, False)
+
+    @branch(is_mid)
+    def _():
+        for j in (2, 3):
+            bz(z_mid, j, z_mid2, False)
+            bz(z_mid, j, z_end, True)
+
+    a_forward(z)
+
+    @branch(is_end)
+    def _():
+        got_az(z_mid2)
+
+    a_own(z_mid2)
+
+    @branch(is_mid)
+    def _():
+        got_az(z_end2)
+        az(z_end2, z_end, True)
+
+    a_forward(near)
+
+    @branch(is_mid)
+    def _():
+        for j in range(4):
+            got_bz(z_end, j)
+            bz(z_end, j, z_mid2, False)
+        for j in range(4):
+            got_bz(z_mid2, j)
+            bz(z_mid2, j, z_end, True)
+
+    @branch(is_end)
+    def _():
+        got_az(z_end2)
+
+    a_own(z_end2)
+    a_forward(z_mid2)
+
+    @branch(is_mid)
+    def _():
+        for j in range(4):
+            got_bz(z_end2, j)
+            bz(z_end2, j, z_end, True)
+
+    for k in range(1, 4):
+        theirs = norms.at[m, pl.ds(((z + 4 - k) % 4) * 4, 4)]
+        remote(theirs, theirs, nm_send.at[2 + k], nm_recv.at[2 + k], line[k - 1]).wait_recv()
+    whole = norms.at[m]
+    copy = remote(whole, whole, nm_send.at[6], nm_recv.at[6], partner)
+    copy.start()
+    tags.append(copy)
+
+    a_forward(z_end2)
+
+    @branch(is_end)
+    def _():
+        for zz in (z_mid, z_mid2, z_end2):
+            for j in range(4):
+                got_bz(zz, j)
+
+    for zz in (z, near, z_mid2, z_end2):
+        got(zz, rd, 0, half_a, AXF + zz)
+        got(zz, rd, half_a, part_a, AYF + zz)
+    theirs = norms.at[1 - m]
+    remote(theirs, theirs, nm_send.at[6], nm_recv.at[6], partner).wait_recv()
+    for copy in small + tags:
+        copy.wait_send()
+    for make in done:
+        make().wait_send()
+    for pred in (is_end, is_mid):
+        @pl.when(pred)
+        def _(pred=pred):
+            for which, copies in tail:
+                if which is pred:
+                    for make in copies:
+                        make().wait_send()
+
+
+def with_kernel(part_a, *args):
+    (tq, dq, sq, tk, dk, sk, tv, dv, sv, norm_train, norm_step) = args
+    fq, fk, fv = stepped(tq, dq, sq), stepped(tk, dk, sk), stepped(tv, dv, sv)
+    norm = norm_train + norm_step
+    length = norm.shape[0]
+    padded = -(-length // LANES) * LANES
+    norm_row = jnp.pad(norm, (0, padded - length)).reshape(1, padded)
+    n, cores = lax.axis_size("fsdp"), lax.axis_size("model")
+    rows = tq.shape[0]
+    wq, wk, wv = tq.shape[1], tk.shape[1], tv.shape[1]
+    width = wq + wk + wv
+    vmem = pl.BlockSpec(memory_space=pltpu.VMEM)
+    held, factor, norms = pl.pallas_call(
+        functools.partial(gather_kernel, part_a),
+        out_shape=(
+            pltpu.VMEM((n, rows, width), jnp.bfloat16),
+            jax.ShapeDtypeStruct((1, width), jnp.float32),
+            jax.ShapeDtypeStruct((cores, n, 1, padded), jnp.float32),
+        ),
+        in_specs=[vmem] * 4,
+        out_specs=(vmem, vmem, vmem),
+        scratch_shapes=[
+            pltpu.VMEM((8, 1, width), jnp.float32),
+            pltpu.SemaphoreType.DMA((6,)),
+            pltpu.SemaphoreType.DMA((6,)),
+            pltpu.SemaphoreType.DMA((7,)),
+            pltpu.SemaphoreType.DMA((7,)),
+            pltpu.SemaphoreType.DMA((COUNT + AX,)),
+            pltpu.SemaphoreType.DMA((COUNT,)),
+        ],
+        compiler_params=pltpu.CompilerParams(
+            collective_id=0, has_side_effects=True, vmem_limit_bytes=24 * 1024 * 1024
+        ),
+    )(fq, fk, fv, norm_row)
+    served = held.reshape(n * rows, width)
+    factor = factor.reshape(width)
+    serve_norm = (
+        norms[:, :, 0, :length].transpose(1, 0, 2).reshape(n * cores * length).astype(jnp.bfloat16)
+    )
+    return (
+        served[:, :wq], served[:, wq : wq + wk], served[:, wq + wk :],
+        factor[:wq], factor[wq : wq + wk], factor[wq + wk :],
+        serve_norm, fq, fk, fv,
+    )
 
 
 def per_device(
@@ -21,6 +352,17 @@
     norm_train,
     norm_step,
 ):
+    n, cores, rows = lax.axis_size("fsdp"), lax.axis_size("model"), train_query.shape[0]
+    part_a = rows - (rows * 2 // 9 // (2 * ROWS)) * 2 * ROWS
+    lanes_ok = all(a.shape[1] % LANES == 0 for a in (train_query, train_key, train_value))
+    if n == 16 and cores == 2 and rows % (2 * ROWS) == 0 and part_a < rows and lanes_ok:
+        return with_kernel(
+            part_a,
+            train_query, drift_query, spread_query,
+            train_key, drift_key, spread_key,
+            train_value, drift_value, spread_value,
+            norm_train, norm_step,
+        )
     fresh_query = train_query - learn_rate * (
         drift_query / (jnp.sqrt(spread_query) + tiny_value) + decay_rate * train_query
     )

time: 371 us -> 149 us (0.40)
  waiting for transfers between devices: 220 us -> 0 us
  Pallas kernels: 0 us -> 120 us
  blocking collectives: 116 us -> 0 us
  between operations: 14 us -> 0.74 us
  local copies, waits for them, and re-layouts: 14.9 us -> 23.2 us
    all_gather x3 -> x0, waiting for transfers between devices: 220 us -> none  [the longest x1 133 us: per_device(): lax.all_gather(narrow_query, 'fsdp', axis=0, tiled=True)]
    pallas_call x0 -> x1, Pallas kernels: none -> 120 us  [with_kernel(): pl.pallas_call(functools.partial(gather_kernel, part_a), out_shape=(pltpu...]
    pmax x1 -> x0, blocking collectives: 78.6 us -> none  [per_device(): lax.pmax((jnp.max(jnp.abs(fresh_query), axis=0), jnp.max(jnp.abs(fresh_ke...]
    unnamed x1 -> x0, blocking collectives: 37.3 us -> none
    slice x0 -> x5, local copies, waits for them, and re-layouts: none -> 16.7 us  [the longest x1 10.3 us: with_kernel(): served[:, :wq]]
    unnamed x37 -> x13, local copies, waits for them, and re-layouts: 14.9 us -> 5.84 us
    sub x0 -> x2, other arithmetic: none -> 3.85 us  [stepped(): train - learn_rate * (drift / (jnp.sqrt(spread) + tiny_value) + decay_rat...]
  transfers between devices with their start and end apart: 3 -> 0, of which waited for: 3 -> 0; matrix products, arithmetic and copies ran while one was open for 1% -> 0% of each run, Pallas kernels for 0% -> 0%
where the time goes in v1:
time: 149 us
  Pallas kernels  120 us (81%)
  local copies, waits for them, and re-layouts  23.2 us (16%)
  other arithmetic  4.53 us (3%)
    pallas_call x1, Pallas kernels, with_kernel(): pl.pallas_call(functools.partial(gather_kernel, part_a), out_shape=(pltpu...  120 us
    slice x1, local copies, waits for them, and re-layouts, with_kernel(): served[:, :wq]  10.3 us
    unnamed x13, local copies, waits for them, and re-layouts  5.84 us
    slice x1, local copies, waits for them, and re-layouts, with_kernel(): served[:, wq + wk:]  5.24 us
    sub x2, other arithmetic, stepped(): train - learn_rate * (drift / (jnp.sqrt(spread) + tiny_value) + decay_rat...  3.85 us

profile of v1, /device:TPU:0, one launch (start us, length us, event | category | flops | bytes accessed | tf_op | source)
XLA Modules:
  0.0 148.9 jit_solution(14705516984458705938)
XLA Ops:
  0.6 0.7 add.33
  1.3 0.0 copy-start.4
  1.3 0.0 copy-start.5
  1.3 1.9 %multiply_subtract_fusion.1 = (f32[160,512]{1,0:T(8,128)S(1)}, f32[160,512]{1,0:T(8,128)S(1)}) fusion(f32[160,512]{1,0:T(8,128)} %param.17, f32[160,512]{1,0:T(8,128)} %param.18, f32[160,512]{1,0:T(8,128)} %param.19, f32[160,512]{1,0:T(8,128)} %param.14, f32[160,512]{1,0:T(8,128)} %param.15, f32[160,512]{1,0:T(8,128)} %param.16), kind=kLoop, calls=%fused_computation.1 | loop fusion | flops 983040 | bytes 2621440 | tf_op jit(solution)/shard_map/sub | solution.py:21
  3.3 0.0 copy-start.2
  3.3 0.0 copy-start.3
  3.3 0.0 copy-done.4
  3.3 0.3 copy-done.5
  3.6 1.9 %multiply_subtract_fusion.fresh_q = f32[160,2048]{1,0:T(8,128)S(1)} fusion(f32[160,2048]{1,0:T(8,128)S(1)} %copy-done.4, f32[160,2048]{1,0:T(8,128)S(1)} %copy-done.5, f32[160,2048]{1,0:T(8,128)} %param.13), kind=kLoop, calls=%fused_computation | loop fusion | flops 1966080 | bytes 5242880 | tf_op jit(solution)/shard_map/sub | solution.py:21
  5.5 0.0 copy-done.2
  5.6 0.0 copy-done.3
  5.6 0.0 copy-start.1
  5.6 120.4 %shard_map.186 = (bf16[16,160,3072]{2,1,0:T(8,128)(2,1)S(1)}, f32[1,3072]{1,0:T(1,128)S(1)}, f32[2,16,1,128]{3,2,1,0:T(1,128)S(1)}) custom-call(f32[160,2048]{1,0:T(8,128)S(1)} %multiply_subtract_fusion.fresh_q, f32[160,512]{1,0:T(8,128)S(1)} %get-tuple-element.21.fresh_k, f32[160,512]{1,0:T(8,128)S(1)} %get-tuple-element.20.fresh_v, ...), custom_call_target="tpu_custom_call" | custom-call | tf_op jit(solution)/shard_map/pallas_call | solution.py:308
  126.0 0.0 copy-start
  126.0 5.5 %copy-done = bf16[16,160,3072]{2,1,0:T(8,128)(2,1)} copy-done((bf16[16,160,3072]{2,1,0:T(8,128)(2,1)}, bf16[16,160,3072]{2,1,0:T(8,128)(2,1)S(1)}, u32[]{:S(2)}) %copy-start) | copy-done | bytes 15728664
  131.5 0.6 fusion.1
  132.1 0.6 slice.34
  132.8 0.7 convert_element_type.14
  133.4 5.2 %fusion = (bf16[2560,512]{1,0:T(8,128)(2,1)}, bf16[2560,512]{1,0:T(8,128)(2,1)}) fusion(bf16[2560,3072]{1,0:T(8,128)(2,1)} %bitcast.11), kind=kLoop, calls=%fused_computation.6 | loop fusion | bytes 10485760 | tf_op jit(solution)/shard_map/slice | solution.py:336
  138.7 0.0 copy-done.1
  138.7 10.3 %slice.41 = bf16[2560,2048]{1,0:T(8,128)(2,1)} slice(bf16[2560,3072]{1,0:T(8,128)(2,1)} %bitcast.12), slice={[0:2560], [0:2048]} | slice | bytes 20971520 | tf_op jit(solution)/shard_map/slice | solution.py:336
  (4 shorter events, 0.0 us)
Async XLA Ops:
  1.3 2.0 %copy-start.4 = (f32[160,2048]{1,0:T(8,128)S(1)}, f32[160,2048]{1,0:T(8,128)}, u32[]{:S(2)}) copy-start(f32[160,2048]{1,0:T(8,128)} %param.11) | copy-start | bytes 3932164
  1.3 2.3 %copy-start.5 = (f32[160,2048]{1,0:T(8,128)S(1)}, f32[160,2048]{1,0:T(8,128)}, u32[]{:S(2)}) copy-start(f32[160,2048]{1,0:T(8,128)} %param.12) | copy-start | bytes 3932164
  3.3 2.3 %copy-start.2 = (f32[160,512]{1,0:T(8,128)}, f32[160,512]{1,0:T(8,128)S(1)}, u32[]{:S(2)}) copy-start(f32[160,512]{1,0:T(8,128)S(1)} %get-tuple-element.20.fresh_v) | copy-start | bytes 983044
  3.3 2.3 %copy-start.3 = (f32[160,512]{1,0:T(8,128)}, f32[160,512]{1,0:T(8,128)S(1)}, u32[]{:S(2)}) copy-start(f32[160,512]{1,0:T(8,128)S(1)} %get-tuple-element.21.fresh_k) | copy-start | bytes 983044
  5.6 133.1 %copy-start.1 = (f32[160,2048]{1,0:T(8,128)}, f32[160,2048]{1,0:T(8,128)S(1)}, u32[]{:S(2)}) copy-start(f32[160,2048]{1,0:T(8,128)S(1)} %multiply_subtract_fusion.fresh_q) | copy-start | bytes 3932164
  126.0 5.5 %copy-start = (bf16[16,160,3072]{2,1,0:T(8,128)(2,1)}, bf16[16,160,3072]{2,1,0:T(8,128)(2,1)S(1)}, u32[]{:S(2)}) copy-start(bf16[16,160,3072]{2,1,0:T(8,128)(2,1)S(1)} %get-tuple-element.13) | copy-start | bytes 47185924

commit v2 on v1

--- a/solution.py
+++ b/solution.py
@@ -12,9 +12,11 @@
 tiny_value = 1e-08
 MESH = pl.DeviceIdType.MESH
 ROWS = 16
+CHUNK = 32
+VMEM_BYTES = 67043328
 LANES = 128
 
-AZ, BZ, AX, AXF, AY, AYF, BX, BXF, BY, BYF, COUNT = 0, 4, 20, 24, 28, 32, 36, 37, 38, 39, 40
+AZ, BZ, AX, AXF, AY, AYF, BXF, BYF, COUNT = 0, 4, 20, 24, 28, 32, 36, 37, 38
 
 
 def stepped(train, drift, spread):
@@ -22,8 +24,11 @@
 
 
 def gather_kernel(
-    part_a, fresh_q, fresh_k, fresh_v, norm_row, held, factor, norms,
-    mx, mx_send, mx_recv, nm_send, nm_recv, send, recv,
+    part_a,
+    tq, dq, sq, tk, dk, sk, tv, dv, sv, norm_train, norm_step,
+    held, fresh_q, fresh_k, fresh_v, factor, norms,
+    in_q, in_k, in_v, norm_in, top, early_q, early_k, early_v,
+    mx, in_sem, norm_sem, mx_send, mx_recv, nm_send, nm_recv, early_send, early_recv, send, recv,
 ):
     f = lax.axis_index("fsdp")
     m = lax.axis_index("model")
@@ -36,6 +41,9 @@
     widths = (fresh_q.shape[1], fresh_k.shape[1], fresh_v.shape[1])
     starts = (0, widths[0], widths[0] + widths[1])
     fresh = (fresh_q, fresh_k, fresh_v)
+    early = (early_q, early_k, early_v)
+    inputs = ((tq, dq, sq), (tk, dk, sk), (tv, dv, sv))
+    local = (in_q, in_k, in_v)
     half_a = part_a // 2
     half_b = (rows - part_a) // 2
 
@@ -50,14 +58,49 @@
     for peer in plane + line + [partner]:
         pl.semaphore_signal(barrier, inc=1, device_id=peer, device_id_type=MESH)
 
-    for ref, start, width in zip(fresh, starts, widths):
-        step = min(512, width)
-        for c in range(0, width, step):
-            def body(i, acc, ref=ref, c=c, step=step):
-                return jnp.maximum(acc, jnp.abs(ref[pl.ds(i * 8, 8), c : c + step]))
-            acc = lax.fori_loop(0, rows // 8, body, jnp.zeros((8, step), jnp.float32), unroll=4)
-            mx[0, :, start + c : start + c + step] = jnp.max(acc, axis=0, keepdims=True)
-    norms[m, f] = norm_row[...]
+    def loads(i):
+        at = pl.ds(pl.multiple_of(i * CHUNK, CHUNK), CHUNK)
+        return [
+            pltpu.make_async_copy(src.at[at], local[a].at[k, at], in_sem.at[i, a * 3 + k])
+            for a in range(3)
+            for k, src in enumerate(inputs[a])
+        ]
+
+    for i in range(rows // CHUNK):
+        for copy in loads(i):
+            copy.start()
+    norm_loads = [
+        pltpu.make_async_copy(src, norm_in.at[k], norm_sem.at[k])
+        for k, src in enumerate((norm_train, norm_step))
+    ]
+    for copy in norm_loads:
+        copy.start()
+
+    top[...] = jnp.zeros_like(top)
+
+    def chunk(i, carry):
+        copies = loads(i)
+        for a, (ref, start, width) in enumerate(zip(fresh, starts, widths)):
+            for copy in copies[a * 3 : a * 3 + 3]:
+                copy.wait()
+            step = min(512, width)
+            for c in range(0, width, step):
+                cols = slice(c, c + step)
+                best = top[:, start + c : start + c + step]
+                for g in range(CHUNK // 8):
+                    at = pl.ds(pl.multiple_of(i * CHUNK + g * 8, 8), 8)
+                    new = stepped(local[a][0, at, cols], local[a][1, at, cols], local[a][2, at, cols])
+                    ref[at, cols] = new
+                    best = jnp.maximum(best, jnp.abs(new))
+                top[:, start + c : start + c + step] = best
+        return carry
+
+    lax.fori_loop(0, rows // CHUNK, chunk, 0)
+    mx[0] = jnp.max(top[...], axis=0, keepdims=True)
+    for copy in norm_loads:
+        copy.wait()
+    norms[m, f] = jnp.zeros_like(norms[m, f])
+    norms[m, f, :, : norm_in.shape[2]] = norm_in[0] + norm_in[1]
 
     pl.semaphore_wait(barrier, 7)
 
@@ -76,6 +119,15 @@
         copy = remote(norms.at[m, f], norms.at[m, f], nm_send.at[k], nm_recv.at[k], peer)
         copy.start()
         tags.append(copy)
+    ahead = []
+    for k in range(2):
+        for a in range(3):
+            copy = remote(
+                fresh[a].at[pl.ds(part_a, rows - part_a)], early[a].at[k],
+                early_send.at[k * 3 + a], early_recv.at[k * 3 + a], plane[k],
+            )
+            copy.start()
+            ahead.append(copy)
     for copy in small:
         copy.wait_recv()
     mx[4] = jnp.maximum(jnp.maximum(mx[0], mx[1]), jnp.maximum(mx[2], mx[3]))
@@ -95,15 +147,16 @@
         copy.wait_recv()
     factor[...] = jnp.maximum(jnp.maximum(mx[4], mx[5]), jnp.maximum(mx[6], mx[7]))
 
-    def narrow(first, last):
+    def narrow(refs, skip, block, first, last):
         def body(i, carry):
             at = pl.ds(pl.multiple_of(first + i * ROWS, ROWS), ROWS)
-            for ref, start, width in zip(fresh, starts, widths):
+            here = pl.ds(pl.multiple_of(first - skip + i * ROWS, ROWS), ROWS)
+            for ref, start, width in zip(refs, starts, widths):
                 step = min(512, width)
                 for c in range(0, width, step):
                     scale = factor[:, start + c : start + c + step]
-                    held[f, at, start + c : start + c + step] = (
-                        ref[at, c : c + step] / scale
+                    held[block, at, start + c : start + c + step] = (
+                        ref[here, c : c + step] / scale
                     ).astype(jnp.bfloat16)
             return carry
         lax.fori_loop(0, (last - first) // ROWS, body, 0)
@@ -157,10 +210,7 @@
         got(zz, ry, 0, part_a, AY + zz)
         go(lambda: copy_of(zz, ry, 0, half_a, AXF + zz, AXF + zz, plane[0]))
 
-    narrow(part_a, rows)
-    go(lambda: copy_of(z, r, part_a, rows, BX, BX, plane[0]))
-    go(lambda: copy_of(z, r, part_a, rows, BY, BY, plane[1]))
-    narrow(0, part_a)
+    narrow(fresh, 0, f, 0, part_a)
 
     tail = []
 
@@ -186,9 +236,13 @@
         az(z_mid, z_end, True)
 
     a_own(z)
-    got(z, rx, part_a, rows, BX)
-    go(lambda: copy_of(z, rx, part_a + half_b, rows, BYF, BYF, plane[1]))
-    got(z, ry, part_a, rows, BY)
+    narrow(fresh, 0, f, part_a, rows)
+    for k, rr in enumerate((rx, ry)):
+        for copy in ahead[k * 3 : k * 3 + 3]:
+            copy.wait_recv()
+        narrow([ref.at[k] for ref in early], part_a, z * 4 + rr, part_a, rows)
+        if k == 0:
+            go(lambda: copy_of(z, rx, part_a + half_b, rows, BYF, BYF, plane[1]))
     go(lambda: copy_of(z, ry, part_a, part_a + half_b, BXF, BXF, plane[0]))
 
     @branch(is_end)
@@ -280,7 +334,7 @@
         got(zz, rd, half_a, part_a, AYF + zz)
     theirs = norms.at[1 - m]
     remote(theirs, theirs, nm_send.at[6], nm_recv.at[6], partner).wait_recv()
-    for copy in small + tags:
+    for copy in small + tags + ahead:
         copy.wait_send()
     for make in done:
         make().wait_send()
@@ -293,49 +347,93 @@
                         make().wait_send()
 
 
+def write_kernel(held, fresh_q, fresh_k, fresh_v, factor, *rest):
+    serve, rates, fresh_out, sems = rest[:3], rest[3:6], rest[6:9], rest[9]
+    n = held.shape[0]
+    cut = max(1, n // 4)
+    copies = []
+    start = 0
+    for k in range(3):
+        width = serve[k].shape[2]
+        for b in range(0, n, cut):
+            copies.append((held.at[pl.ds(b, cut), :, pl.ds(start, width)], serve[k].at[pl.ds(b, cut)]))
+        copies.append((factor.at[:, pl.ds(start, width)], rates[k]))
+        copies.append(((fresh_q, fresh_k, fresh_v)[k], fresh_out[k]))
+        start += width
+    copies = [pltpu.make_async_copy(src, dst, sems.at[i]) for i, (src, dst) in enumerate(copies)]
+    for copy in copies:
+        copy.start()
+    for copy in copies:
+        copy.wait()
+
+
 def with_kernel(part_a, *args):
     (tq, dq, sq, tk, dk, sk, tv, dv, sv, norm_train, norm_step) = args
-    fq, fk, fv = stepped(tq, dq, sq), stepped(tk, dk, sk), stepped(tv, dv, sv)
-    norm = norm_train + norm_step
-    length = norm.shape[0]
+    length = norm_train.shape[0]
     padded = -(-length // LANES) * LANES
-    norm_row = jnp.pad(norm, (0, padded - length)).reshape(1, padded)
     n, cores = lax.axis_size("fsdp"), lax.axis_size("model")
     rows = tq.shape[0]
-    wq, wk, wv = tq.shape[1], tk.shape[1], tv.shape[1]
-    width = wq + wk + wv
+    widths = (tq.shape[1], tk.shape[1], tv.shape[1])
+    width = sum(widths)
     vmem = pl.BlockSpec(memory_space=pltpu.VMEM)
-    held, factor, norms = pl.pallas_call(
+    hbm = pl.BlockSpec(memory_space=pltpu.HBM)
+    f32, bf16 = jnp.float32, jnp.bfloat16
+    room = VMEM_BYTES - n * rows * width * 2 - rows * width * 4 - 192 * 1024
+    held, fresh_q, fresh_k, fresh_v, factor, norms = pl.pallas_call(
         functools.partial(gather_kernel, part_a),
         out_shape=(
-            pltpu.VMEM((n, rows, width), jnp.bfloat16),
-            jax.ShapeDtypeStruct((1, width), jnp.float32),
-            jax.ShapeDtypeStruct((cores, n, 1, padded), jnp.float32),
+            pltpu.VMEM((n, rows, width), bf16),
+            *[pltpu.VMEM((rows, w), f32) for w in widths],
+            pltpu.VMEM((1, width), f32),
+            jax.ShapeDtypeStruct((cores, n, 1, padded), f32),
         ),
-        in_specs=[vmem] * 4,
-        out_specs=(vmem, vmem, vmem),
+        in_specs=[hbm] * 11,
+        out_specs=(vmem,) * 6,
         scratch_shapes=[
-            pltpu.VMEM((8, 1, width), jnp.float32),
+            *[pltpu.VMEM((3, rows, w), f32) for w in widths],
+            pltpu.VMEM((2, 1, length), f32),
+            pltpu.VMEM((8, width), f32),
+            *[pltpu.VMEM((2, rows - part_a, w), f32) for w in widths],
+            pltpu.VMEM((8, 1, width), f32),
+            pltpu.SemaphoreType.DMA((rows // CHUNK, 9)),
+            pltpu.SemaphoreType.DMA((2,)),
             pltpu.SemaphoreType.DMA((6,)),
             pltpu.SemaphoreType.DMA((6,)),
             pltpu.SemaphoreType.DMA((7,)),
             pltpu.SemaphoreType.DMA((7,)),
+            pltpu.SemaphoreType.DMA((6,)),
+            pltpu.SemaphoreType.DMA((6,)),
             pltpu.SemaphoreType.DMA((COUNT + AX,)),
             pltpu.SemaphoreType.DMA((COUNT,)),
         ],
         compiler_params=pltpu.CompilerParams(
-            collective_id=0, has_side_effects=True, vmem_limit_bytes=24 * 1024 * 1024
+            collective_id=0, has_side_effects=True, vmem_limit_bytes=room
         ),
-    )(fq, fk, fv, norm_row)
-    served = held.reshape(n * rows, width)
-    factor = factor.reshape(width)
+        name="gather",
+    )(
+        tq, dq, sq, tk, dk, sk, tv, dv, sv,
+        norm_train.reshape(1, length), norm_step.reshape(1, length),
+    )
+    out = pl.pallas_call(
+        write_kernel,
+        out_shape=(
+            *[jax.ShapeDtypeStruct((n, rows, w), bf16) for w in widths],
+            *[jax.ShapeDtypeStruct((1, w), f32) for w in widths],
+            *[jax.ShapeDtypeStruct((rows, w), f32) for w in widths],
+        ),
+        in_specs=[vmem] * 5,
+        out_specs=(hbm,) * 9,
+        scratch_shapes=[pltpu.SemaphoreType.DMA((18,))],
+        compiler_params=pltpu.CompilerParams(vmem_limit_bytes=4 * 1024 * 1024),
+        name="write",
+    )(held, fresh_q, fresh_k, fresh_v, factor)
     serve_norm = (
-        norms[:, :, 0, :length].transpose(1, 0, 2).reshape(n * cores * length).astype(jnp.bfloat16)
+        norms[:, :, 0, :length].transpose(1, 0, 2).reshape(n * cores * length).astype(bf16)
     )
     return (
-        served[:, :wq], served[:, wq : wq + wk], served[:, wq + wk :],
-        factor[:wq], factor[wq : wq + wk], factor[wq + wk :],
-        serve_norm, fq, fk, fv,
+        *[a.reshape(n * rows, w) for a, w in zip(out[:3], widths)],
+        *[a.reshape(w) for a, w in zip(out[3:6], widths)],
+        serve_norm, *out[6:],
     )
 
 
@@ -355,7 +453,7 @@
     n, cores, rows = lax.axis_size("fsdp"), lax.axis_size("model"), train_query.shape[0]
     part_a = rows - (rows * 2 // 9 // (2 * ROWS)) * 2 * ROWS
     lanes_ok = all(a.shape[1] % LANES == 0 for a in (train_query, train_key, train_value))
-    if n == 16 and cores == 2 and rows % (2 * ROWS) == 0 and part_a < rows and lanes_ok:
+    if n == 16 and cores == 2 and rows % CHUNK == 0 and part_a < rows and lanes_ok:
         return with_kernel(
             part_a,
             train_query, drift_query, spread_query,

time: 149 us -> 129 us (0.87)
  local copies, waits for them, and re-layouts: 23.2 us -> 0.71 us
  Pallas kernels: 120 us -> 128 us
  other arithmetic: 4.53 us -> 0 us
    slice x4 -> x0, local copies, waits for them, and re-layouts: 16.7 us -> none  [the longest x1 10.3 us: with_kernel(): served[:, :wq]]
    pallas_call x0 -> x1, Pallas kernels: none -> 6.27 us  [with_kernel(): pl.pallas_call(write_kernel, out_shape=(*[jax.ShapeDtypeStruct((n, rows,...]
    unnamed x13 -> x3, local copies, waits for them, and re-layouts: 5.84 us -> 0.01 us
    sub x2 -> x0, other arithmetic: 3.85 us -> none  [stepped(): train - learn_rate * (drift / (jnp.sqrt(spread) + tiny_value) + decay_rat...]
where the time goes in v2:
time: 129 us
  Pallas kernels  128 us (99%)
    pallas_call x1, Pallas kernels, with_kernel(): pl.pallas_call(functools.partial(gather_kernel, part_a), out_shape=(pltpu...  122 us
    pallas_call x1, Pallas kernels, with_kernel(): pl.pallas_call(write_kernel, out_shape=(*[jax.ShapeDtypeStruct((n, rows,...  6.27 us

profile of v2, /device:TPU:0, one launch (start us, length us, event | category | flops | bytes accessed | tf_op | source)
XLA Modules:
  0.0 129.2 jit_solution(1660080170916957855)
XLA Ops:
  0.6 121.6 %gather.1 = (bf16[16,160,3072]{2,1,0:T(8,128)(2,1)S(1)}, f32[160,2048]{1,0:T(8,128)S(1)}, f32[160,512]{1,0:T(8,128)S(1)}, f32[160,512]{1,0:T(8,128)S(1)}, f32[1,...) custom-call(f32[160,2048]{1,0:T(8,128)} %tq.1, f32[160,2048]{1,0:T(8,128)} %dq.1, f32[160,2048]{1,0:T(8,128)} %sq.1, ...), custom_call_target="tpu_custom_call" | custom-call | tf_op jit(solution)/shard_map/gather/pallas_call | solution.py:382
  122.2 0.0 copy-start
  122.2 6.3 %write.1 = (bf16[16,160,2048]{2,1,0:T(8,128)(2,1)}, bf16[16,160,512]{2,1,0:T(8,128)(2,1)}, bf16[16,160,512]{2,1,0:T(8,128)(2,1)}, f32[1,2048]{1,0:T(1,128)}, f32...) custom-call(bf16[16,160,3072]{2,1,0:T(8,128)(2,1)S(1)} %get-tuple-elemen, ...), custom_call_target="tpu_custom_call" | custom-call | tf_op jit(solution)/shard_map/write/pallas_call | solution.py:417
  128.5 0.0 copy-done
  128.6 0.7 convert_element_type.12
  (3 shorter events, 0.0 us)
Async XLA Ops:
  122.2 6.3 %copy-start = (f32[2,16,1,128]{3,2,1,0:T(1,128)S(1)}, f32[2,16,1,128]{3,2,1,0:T(1,128)}, u32[]{:S(2)}) copy-start(f32[2,16,1,128]{3,2,1,0:T(1,128)} %get-tuple-element.36) | copy-start | bytes 49156
